TPU v7x, 128 devices: a whole 4x4x4 slice. The times are simulated.
128 devices in a mesh: bank: 4 (over x_lo, core), zero: 32 (over z, y, x_hi).
Axes of the slice: x: 4 (x_hi: 2, x_lo: 2; x = x_hi * 2 + x_lo), y: 4, z: 4, core: 2. Of those that a mesh axis runs over, the one named last changes fastest.
Arguments:
- w_gate: float32 [64, 2048, 1024], P('bank', 'zero'), may hold values from -0.25 to 0.25
- avg_gate: float32 [64, 2048, 1024], P('bank', 'zero'), may hold values from -0.125 to 0.125
- w_up: float32 [64, 2048, 1024], P('bank', 'zero'), may hold values from -0.25 to 0.25
- avg_up: float32 [64, 2048, 1024], P('bank', 'zero'), may hold values from -0.125 to 0.125
- mix_share: float32 [64], P('bank'), may hold values from 0.2 to 0.8
- router_weight: float32 [2048, 64], P('zero', 'bank'), may hold values from -0.125 to 0.125
- router_gain: float32 [2048], P('zero'), may hold values from 0.25 to 1.75
Outputs:
- serve_gate: bfloat16 [64, 2048, 1024], P('bank', None, 'zero')
- serve_up: bfloat16 [64, 2048, 1024], P('bank', None, 'zero')
- scale_gate: float32 [64, 1024], P('bank', 'zero')
- scale_up: float32 [64, 1024], P('bank', 'zero')
- serve_router: bfloat16 [2048, 64], replicated
All inputs are finite; a program needn't handle non-finite values. Where the computation divides by a largest or mean magnitude, that divisor is 1e-20 or more.
Results may differ from a plain program's by a relative error of at most 0.001.
Values may be sent and summed in bfloat16 or wider, within the bound.
A program may use at most 128 MiB of HBM per device.

v0:
```python
import jax
import jax.numpy as jnp
from jax import lax
from jax.sharding import PartitionSpec as P

D_MODEL = 2048


def filled_up(lines, size):
    spare = -len(lines) % size
    return jnp.pad(lines, [(0, spare)] + [(0, 0)] * (lines.ndim - 1))


def from_everyone(array, axis):
    copies = jnp.broadcast_to(array, (lax.axis_size(axis), *array.shape))
    return lax.all_to_all(copies, axis, split_axis=0, concat_axis=0, tiled=True)


def laid_out(blocks, dim):
    dims = list(blocks.shape[1:])
    dims[dim] *= blocks.shape[0]
    return jnp.moveaxis(blocks, 0, dim).reshape(dims)


def collect(array, axis, dim):
    blocks = from_everyone(array, axis)
    return laid_out(blocks, dim)


def split_up(array, dim, size):
    dims = array.shape
    blocks = array.reshape(*dims[:dim], size, dims[dim] // size, *dims[dim + 1 :])
    return jnp.moveaxis(blocks, dim, 0)


def sent_and_summed(array, axis, dim):
    size = lax.axis_size(axis)
    blocks = lax.all_to_all(split_up(array, dim, size), axis, 0, 0, tiled=True)
    return jnp.sum(blocks, axis=0)


def sum_by_parts(array, axes):
    padded = filled_up(array, lax.axis_size(axes))
    whole = collect(sent_and_summed(padded, axes, 0), axes, 0)
    return lax.slice_in_dim(whole, 0, len(array)).reshape(array.shape)


def together(arrays, axis):
    vector, at, gathered = (jnp.concatenate([a.reshape(-1) for a in arrays]), 0, [])
    subtotal = sum_by_parts(vector, axis)
    for a in arrays:
        gathered.append(subtotal[at : at + a.size].reshape(a.shape))
        at += a.size
    return tuple(gathered)


def on_device(w_gate, avg_gate, w_up, avg_up, mix_share, router_weight, router_gain):
    fresh_gate = mix_share[:, None, None] * w_gate + (1.0 - mix_share[:, None, None]) * avg_gate
    fresh_up = mix_share[:, None, None] * w_up + (1.0 - mix_share[:, None, None]) * avg_up
    total_gate, total_up = together(
        (jnp.sum(jnp.abs(fresh_gate), axis=1), jnp.sum(jnp.abs(fresh_up), axis=1)), "zero"
    )
    scale_gate = total_gate / D_MODEL
    scale_up = total_up / D_MODEL
    narrow_gate, narrow_up = (
        (fresh_gate / jnp.expand_dims(scale_gate, 1)).astype(jnp.bfloat16),
        (fresh_up / jnp.expand_dims(scale_up, 1)).astype(jnp.bfloat16),
    )
    serve_gate, serve_up = (
        lax.all_to_all(narrow_gate, "zero", split_axis=2, concat_axis=1, tiled=True),
        lax.all_to_all(narrow_up, "zero", split_axis=2, concat_axis=1, tiled=True),
    )
    scale_gate = lax.dynamic_slice_in_dim(
        scale_gate, lax.axis_index("zero") * serve_gate.shape[2], serve_gate.shape[2], axis=1
    )
    scale_up = lax.dynamic_slice_in_dim(
        scale_up, lax.axis_index("zero") * serve_up.shape[2], serve_up.shape[2], axis=1
    )
    part_router = (router_weight * router_gain[:, None]).astype(jnp.bfloat16)
    row_router = collect(part_router, "zero", 0)
    serve_router = collect(row_router, "bank", 1)
    return (serve_gate, serve_up, scale_gate, scale_up, serve_router)


def solution(mesh):
    in_specs = (
        P("bank", "zero", None),
        P("bank", "zero", None),
        P("bank", "zero", None),
        P("bank", "zero", None),
        P("bank"),
        P("zero", "bank"),
        P("zero"),
    )
    out_specs = (
        P("bank", None, "zero"),
        P("bank", None, "zero"),
        P("bank", "zero"),
        P("bank", "zero"),
        P(),
    )
    return jax.shard_map(
        on_device, mesh=mesh, in_specs=in_specs, out_specs=out_specs, check_vma=False
    )
```

profile of v0, /device:TPU:0, one launch (start us, length us, event | category | flops | bytes accessed | tf_op | source)
XLA Modules:
  0.0 181.1 jit_solution(16455690182779378878)
XLA Ops:
  0.6 0.7 broadcast_subtract_fusion
  1.3 0.0 copy-start
  1.3 0.0 copy-start.2
  1.3 0.0 copy-start.1
  1.3 8.4 %abs_reduce_fusion.1 = (f32[16,1024]{1,0:T(8,128)S(1)}, f32[16,1024]{1,0:T(8,128)S(1)}) fusion(f32[16,64,1024]{2,1,0:T(8,128)} %param.8, f32[16]{0:T(128)S(1)} %broadcast_subtract_fusion, f32[16,64,1024]{2,1,0:T(8,128)} %param.7, f32[16]{0:T(128)} %param.11, f32[16,64,1024]{2,1,0:T(8,128)} %param.10, f32[16,64,1024]{2,1,0:T(8,128)} %param.9), kind=kLoop, calls=%fused_computation.4 | loop fusion | flops 10452992 | bytes 16908416 | tf_op jit(solution)/shard_map/reduce_sum | solution.py:61
  9.8 0.7 all_to_all.42
  10.5 10.9 %all-to-all-start = ((f32[32,1,1024]{2,1,0:T(1,128)}), f32[32,1,1024]{2,1,0:T(1,128)S(1)}, u32[]{:S(2)}, u32[]{:S(2)}) async-start(f32[32,1,1024]{2,1,0:T(1,128)} %all_to_all.42), calls=%async_computation | async-start | bytes 262144 | tf_op jit(solution)/shard_map/all_to_all | solution.py:38
  21.4 0.0 copy-done
  21.4 0.0 copy-done.2
  21.5 0.8 reshape.56
  22.3 9.4 %all-to-all-done = f32[32,1,1024]{2,1,0:T(1,128)S(1)} async-done(((f32[32,1,1024]{2,1,0:T(1,128)}), f32[32,1,1024]{2,1,0:T(1,128)S(1)}, u32[]{:S(2)}, u32[]{:S(2)}) %all-to-all-start) | async-done | bytes 131104 | tf_op jit(solution)/shard_map/all_to_all | solution.py:38
  31.7 3.9 %all-to-all-start.4 = ((bf16[32,2,512]{2,1,0:T(2,128)(2,1)}), bf16[32,2,512]{2,1,0:T(2,128)(2,1)S(1)}, u32[]{:S(2)}, u32[]{:S(2)}) async-start(bf16[32,2,512]{2,1,0:T(2,128)(2,1)} %reshape.56), calls=%async_computation.4 | async-start | bytes 131072 | tf_op jit(solution)/shard_map/all_to_all | solution.py:16
  35.5 0.1 reduce_sum.29
  35.6 9.8 %all-to-all-done.4 = bf16[32,2,512]{2,1,0:T(2,128)(2,1)S(1)} async-done(((bf16[32,2,512]{2,1,0:T(2,128)(2,1)}), bf16[32,2,512]{2,1,0:T(2,128)(2,1)S(1)}, u32[]{:S(2)}, u32[]{:S(2)}) %all-to-all-start.4) | async-done | bytes 65568 | tf_op jit(solution)/shard_map/all_to_all | solution.py:16
  45.4 0.7 broadcast_in_dim.6
  46.1 3.9 %all-to-all-start.1 = ((f32[32,1,1024]{2,1,0:T(1,128)}), f32[32,1,1024]{2,1,0:T(1,128)S(1)}, u32[]{:S(2)}, u32[]{:S(2)}) async-start(f32[32,1,1024]{2,1,0:T(1,128)} %broadcast_in_dim.6), calls=%async_computation.1 | async-start | bytes 262144 | tf_op jit(solution)/shard_map/all_to_all | solution.py:16
  50.0 0.1 reshape.57
  50.2 0.2 reshape.50
  50.4 9.8 %all-to-all-done.1 = f32[32,1,1024]{2,1,0:T(1,128)S(1)} async-done(((f32[32,1,1024]{2,1,0:T(1,128)}), f32[32,1,1024]{2,1,0:T(1,128)S(1)}, u32[]{:S(2)}, u32[]{:S(2)}) %all-to-all-start.1) | async-done | bytes 131104 | tf_op jit(solution)/shard_map/all_to_all | solution.py:16
  60.2 0.7 broadcast_in_dim.8
  60.9 3.4 %all-to-all-start.5 = ((bf16[4,2048,16]{1,2,0:T(8,128)(2,1)}), bf16[4,2048,16]{1,2,0:T(8,128)(2,1)S(1)}, u32[]{:S(2)}, u32[]{:S(2)}) async-start(bf16[4,2048,16]{1,2,0:T(8,128)(2,1)} %broadcast_in_dim.8), calls=%async_computation.5 | async-start | bytes 524288 | tf_op jit(solution)/shard_map/all_to_all | solution.py:16
  64.3 0.1 slice_multiply_fusion
  64.5 0.0 copy-done.1
  64.5 8.3 %divide_convert_fusion = (bf16[16,64,1024]{2,1,0:T(8,128)(2,1)}, bf16[16,64,1024]{2,1,0:T(8,128)(2,1)S(1)}) fusion(f32[16,1024]{1,0:T(8,128)S(1)} %get-tuple-element.11, f32[16,64,1024]{2,1,0:T(8,128)} %param.10, f32[16]{0:T(128)S(1)} %broadcast_subtract_fusion, f32[16,64,1024]{2,1,0:T(8,128)} %param.9, f32[16]{0:T(128)S(1)} %copy-done.1, ...), kind=kLoop, calls=%fused_computation | loop fusion | flops 10485760 | bytes 21102720 | tf_op jit(solution)/shard_map/convert_element_type | solution.py:67
  72.8 4.9 %copy.74 = bf16[16,64,1024]{1,0,2:T(8,128)(2,1)} copy(bf16[16,64,1024]{2,1,0:T(8,128)(2,1)S(1)} %get-tuple-element.10) | data formatting | bytes 4194304 | tf_op jit(solution)/shard_map/convert_element_type | solution.py:66
  77.7 7.9 %reshape.52 = bf16[32,2,16384]{2,1,0:T(2,128)(2,1)} reshape(bf16[1024,16,64]{2,1,0:T(8,128)(2,1)} %bitcast.32) | data formatting | bytes 4194304
  85.6 0.0 all-to-all-done.5
  85.6 4.0 %all-to-all-start.2 = ((bf16[32,2,16384]{2,1,0:T(2,128)(2,1)}), bf16[32,2,16384]{2,1,0:T(2,128)(2,1)S(1)}, u32[]{:S(2)}, u32[]{:S(2)}) async-start(bf16[32,2,16384]{2,1,0:T(2,128)(2,1)} %reshape.52), calls=%async_computation.2 | async-start | bytes 4194304 | tf_op jit(solution)/shard_map/all_to_all | solution.py:70
  89.6 6.2 %copy.77 = bf16[16,64,1024]{1,0,2:T(8,128)(2,1)} copy(bf16[16,64,1024]{2,1,0:T(8,128)(2,1)} %get-tuple-element.9) | data formatting | bytes 4194304 | tf_op jit(solution)/shard_map/convert_element_type | solution.py:67
  95.8 7.9 %reshape.54 = bf16[32,2,16384]{2,1,0:T(2,128)(2,1)} reshape(bf16[1024,16,64]{2,1,0:T(8,128)(2,1)} %bitcast.33) | data formatting | bytes 4194304
  103.7 17.5 %all-to-all-done.2 = bf16[32,2,16384]{2,1,0:T(2,128)(2,1)S(1)} async-done(((bf16[32,2,16384]{2,1,0:T(2,128)(2,1)}), bf16[32,2,16384]{2,1,0:T(2,128)(2,1)S(1)}, u32[]{:S(2)}, u32[]{:S(2)}) %all-to-all-start.2) | async-done | bytes 2097184 | tf_op jit(solution)/shard_map/all_to_all | solution.py:70
  121.1 8.1 %all-to-all-start.3 = ((bf16[32,2,16384]{2,1,0:T(2,128)(2,1)}), bf16[32,2,16384]{2,1,0:T(2,128)(2,1)}, u32[]{:S(2)}, u32[]{:S(2)}) async-start(bf16[32,2,16384]{2,1,0:T(2,128)(2,1)} %reshape.54), calls=%async_computation.3 | async-start | bytes 4194304 | tf_op jit(solution)/shard_map/all_to_all | solution.py:71
  129.2 0.7 constant_dynamic-slice_fusion
  129.9 4.0 %reshape.53 = bf16[1024,16,64]{2,1,0:T(8,128)(2,1)} reshape(bf16[32,2,16384]{2,1,0:T(2,128)(2,1)S(1)} %all-to-all-done.2) | data formatting | bytes 4194304
  133.9 6.9 %copy.76 = bf16[16,32,64,32]{2,1,3,0:T(8,128)(2,1)} copy(bf16[16,32,64,32]{2,0,3,1:T(8,128)(2,1)} %bitcast.34) | data formatting | bytes 4194304 | tf_op jit(solution)/shard_map/all_to_all | solution.py:70
  140.8 6.7 %all_to_all.48 = bf16[16,2048,32]{1,2,0:T(8,128)(2,1)} reshape(bf16[16,32,64,32]{2,1,3,0:T(8,128)(2,1)} %copy.76) | data formatting | bytes 4194304 | tf_op jit(solution)/shard_map/all_to_all | solution.py:70
  147.5 11.3 %all-to-all-done.3 = bf16[32,2,16384]{2,1,0:T(2,128)(2,1)} async-done(((bf16[32,2,16384]{2,1,0:T(2,128)(2,1)}), bf16[32,2,16384]{2,1,0:T(2,128)(2,1)}, u32[]{:S(2)}, u32[]{:S(2)}) %all-to-all-start.3) | async-done | bytes 2097184 | tf_op jit(solution)/shard_map/all_to_all | solution.py:71
  158.9 7.9 %reshape.55 = bf16[1024,16,64]{2,1,0:T(8,128)(2,1)} reshape(bf16[32,2,16384]{2,1,0:T(2,128)(2,1)} %all-to-all-done.3) | data formatting | bytes 4194304
  166.8 6.9 %copy.79 = bf16[16,32,64,32]{2,1,3,0:T(8,128)(2,1)} copy(bf16[16,32,64,32]{2,0,3,1:T(8,128)(2,1)} %bitcast.35) | data formatting | bytes 4194304 | tf_op jit(solution)/shard_map/all_to_all | solution.py:71
  173.7 6.7 %all_to_all.52 = bf16[16,2048,32]{1,2,0:T(8,128)(2,1)} reshape(bf16[16,32,64,32]{2,1,3,0:T(8,128)(2,1)} %copy.79) | data formatting | bytes 4194304 | tf_op jit(solution)/shard_map/all_to_all | solution.py:71
  180.4 0.7 copy.90
  (5 shorter events, 0.1 us)
Async XLA Ops:
  1.3 20.1 %copy-start = (f32[64,16]{0,1:T(8,128)S(1)}, f32[64,16]{0,1:T(8,128)}, u32[]{:S(2)}) copy-start(f32[64,16]{0,1:T(8,128)} %param.12) | copy-start | bytes 12292
  1.3 20.1 %copy-start.2 = (f32[64]{0:T(128)S(1)}, f32[64]{0:T(128)}, u32[]{:S(2)}) copy-start(f32[64]{0:T(128)} %param.13) | copy-start | bytes 772
  1.3 63.2 %copy-start.1 = (f32[16]{0:T(128)S(1)}, f32[16]{0:T(128)}, u32[]{:S(2)}) copy-start(f32[16]{0:T(128)} %param.11) | copy-start | bytes 196
  10.5 21.1 %all-to-all-start = ((f32[32,1,1024]{2,1,0:T(1,128)}), f32[32,1,1024]{2,1,0:T(1,128)S(1)}, u32[]{:S(2)}, u32[]{:S(2)}) async-start(f32[32,1,1024]{2,1,0:T(1,128)} %all_to_all.42), calls=%async_computation | async-start | bytes 262144 | tf_op jit(solution)/shard_map/all_to_all | solution.py:38
  31.7 13.7 %all-to-all-start.4 = ((bf16[32,2,512]{2,1,0:T(2,128)(2,1)}), bf16[32,2,512]{2,1,0:T(2,128)(2,1)S(1)}, u32[]{:S(2)}, u32[]{:S(2)}) async-start(bf16[32,2,512]{2,1,0:T(2,128)(2,1)} %reshape.56), calls=%async_computation.4 | async-start | bytes 131072 | tf_op jit(solution)/shard_map/all_to_all | solution.py:16
  46.1 14.1 %all-to-all-start.1 = ((f32[32,1,1024]{2,1,0:T(1,128)}), f32[32,1,1024]{2,1,0:T(1,128)S(1)}, u32[]{:S(2)}, u32[]{:S(2)}) async-start(f32[32,1,1024]{2,1,0:T(1,128)} %broadcast_in_dim.6), calls=%async_computation.1 | async-start | bytes 262144 | tf_op jit(solution)/shard_map/all_to_all | solution.py:16
  60.9 24.7 %all-to-all-start.5 = ((bf16[4,2048,16]{1,2,0:T(8,128)(2,1)}), bf16[4,2048,16]{1,2,0:T(8,128)(2,1)S(1)}, u32[]{:S(2)}, u32[]{:S(2)}) async-start(bf16[4,2048,16]{1,2,0:T(8,128)(2,1)} %broadcast_in_dim.8), calls=%async_computation.5 | async-start | bytes 524288 | tf_op jit(solution)/shard_map/all_to_all | solution.py:16
  85.6 35.5 %all-to-all-start.2 = ((bf16[32,2,16384]{2,1,0:T(2,128)(2,1)}), bf16[32,2,16384]{2,1,0:T(2,128)(2,1)S(1)}, u32[]{:S(2)}, u32[]{:S(2)}) async-start(bf16[32,2,16384]{2,1,0:T(2,128)(2,1)} %reshape.52), calls=%async_computation.2 | async-start | bytes 4194304 | tf_op jit(solution)/shard_map/all_to_all | solution.py:70
  121.1 37.8 %all-to-all-start.3 = ((bf16[32,2,16384]{2,1,0:T(2,128)(2,1)}), bf16[32,2,16384]{2,1,0:T(2,128)(2,1)}, u32[]{:S(2)}, u32[]{:S(2)}) async-start(bf16[32,2,16384]{2,1,0:T(2,128)(2,1)} %reshape.54), calls=%async_computation.3 | async-start | bytes 4194304 | tf_op jit(solution)/shard_map/all_to_all | solution.py:71
where the time goes:
time: 183 us; the launch traced here: 181 us
  local copies, waits for them, and re-layouts  70.7 us (39%)
  waiting for transfers between devices  57.8 us (32%)
  starting transfers between devices  34.1 us (19%)
  other arithmetic  17.7 us (10%)
    unnamed x15, local copies, waits for them, and re-layouts  29.3 us
    all_to_all x3, waiting for transfers between devices, from_everyone(): return lax.all_to_all(copies, axis, split_axis=0, concat_axis=0, tiled=True)  19.6 us
    all_to_all x1, waiting for transfers between devices, on_device(): lax.all_to_all(narrow_gate, 'zero', split_axis=2, concat_axis=1, tiled=True)  17.5 us
    all_to_all x2, local copies, waits for them, and re-layouts, on_device(): lax.all_to_all(narrow_gate, 'zero', split_axis=2, concat_axis=1, tiled=True)  13.6 us
    all_to_all x2, local copies, waits for them, and re-layouts, on_device(): lax.all_to_all(narrow_up, 'zero', split_axis=2, concat_axis=1, tiled=True)  13.6 us
    all_to_all x1, waiting for transfers between devices, on_device(): lax.all_to_all(narrow_up, 'zero', split_axis=2, concat_axis=1, tiled=True)  11.3 us
    all_to_all x3, starting transfers between devices, from_everyone(): return lax.all_to_all(copies, axis, split_axis=0, concat_axis=0, tiled=True)  11.1 us
    all_to_all x1, starting transfers between devices, sent_and_summed(): blocks = lax.all_to_all(split_up(array, dim, size), axis, 0, 0, tiled=True)  10.9 us
  transfers between devices with their start and end apart: 6, of which 5 were waited for; matrix products, arithmetic and copies ran while one was open for 27% of the time, Pallas kernels for 0%

commit v1 on v0

v1 whole, which is shorter than its diff:
```python
import functools

import jax
import jax.numpy as jnp
from jax import lax
from jax.experimental import pallas as pl
from jax.experimental.pallas import tpu as pltpu
from jax.sharding import PartitionSpec as P

D_MODEL = 2048
EXPERTS = 16
ROWS = 64
WIDTH = 1024
PEERS = 32
SHARE = 32
F32 = jnp.float32
BF16 = jnp.bfloat16
MESH = pl.DeviceIdType.MESH


def peer_order():
    every = [(x, y, z) for z in range(4) for y in range(4) for x in range(2)][1:]
    along_x = [o for o in every if o[0]]
    along_y = [o for o in every if not o[0] and o[1]]
    along_z = [o for o in every if not o[0] and not o[1]]
    order = []
    while along_x or along_y or along_z:
        if along_x:
            order.append(along_x.pop(0))
        if along_y:
            order.append(along_y.pop(0))
        if along_z and (len(order) % 3 == 0 or not (along_x or along_y)):
            order.append(along_z.pop(0))
    return order


ORDER = peer_order()


def place(me, offset):
    x, y, z = offset
    at_z = lax.rem(me // 8 + z, 4)
    at_y = lax.rem(lax.rem(me // 2, 4) + y, 4)
    at_x = lax.rem(lax.rem(me, 2) + x, 2)
    return at_z * 8 + at_y * 2 + at_x


def wait_for(ref, sem):
    pltpu.make_async_copy(ref, ref, sem).wait()


def kernel(
    mix_ref,
    router_ref,
    gain_ref,
    w_gate,
    avg_gate,
    w_up,
    avg_up,
    out_gate,
    out_up,
    out_scale_gate,
    out_scale_up,
    out_router,
    fresh,
    other,
    part,
    part_in,
    total,
    narrow,
    landed,
    near_out,
    near_in,
    far_out,
    far_in,
    load_sem,
    part_sem,
    total_sem,
    bulk_send,
    bulk_recv,
    near_sem,
    far_sem,
):
    me = lax.axis_index("zero")
    bank = lax.axis_index("bank")
    half = lax.rem(me, 2)
    barrier = pltpu.get_barrier_semaphore()
    peers = [place(me, o) for o in ORDER]
    nearby = [
        (lax.rem(bank + b, 4), me + h * (1 - 2 * half))
        for b in range(4)
        for h in range(2)
        if (b, h) != (0, 0)
    ]
    for peer in peers:
        pl.semaphore_signal(barrier, inc=1, device_id={"zero": peer}, device_id_type=MESH)
    for to_bank, to_zero in nearby:
        pl.semaphore_signal(
            barrier, inc=1, device_id={"bank": to_bank, "zero": to_zero}, device_id_type=MESH
        )

    loads = []
    for t, (w, a) in enumerate(((w_gate, avg_gate), (w_up, avg_up))):
        for q in range(4):
            rows = pl.ds(q * 256, 256)
            pair = []
            for n, (source, target) in enumerate(((w, fresh), (a, other))):
                copy = pltpu.make_async_copy(
                    source.at[rows], target.at[t, rows], load_sem.at[t * 8 + q * 2 + n]
                )
                copy.start()
                pair.append(copy)
            loads.append(pair)

    share = router_ref[...] * gain_ref[...]
    near_out[...] = jnp.concatenate([share, share], axis=1).astype(BF16)

    for t in range(2):
        for q in range(4):
            for copy in loads[t * 4 + q]:
                copy.wait()

            def mean_step(n, carry, t=t, q=q):
                e = q * 4 + n
                mix = mix_ref[e]
                rest = 1.0 - mix
                line = t * EXPERTS + e
                rows = pl.ds(pl.multiple_of(e * ROWS, ROWS), ROWS)
                for c in range(8):
                    lanes = slice(c * 128, c * 128 + 128)
                    value = mix * fresh[t, rows, lanes] + rest * other[t, rows, lanes]
                    fresh[t, rows, lanes] = value
                    part[4 * c + line // 8, pl.ds(lax.rem(line, 8), 1), :] = jnp.sum(
                        jnp.abs(value), axis=0, keepdims=True
                    )
                return carry

            lax.fori_loop(0, 4, mean_step, 0)

    pl.semaphore_wait(barrier, len(peers) + len(nearby))

    sends = []
    for peer in peers:
        copy = pltpu.make_async_remote_copy(
            part.at[peer], part_in.at[me], part_sem.at[0], part_sem.at[1],
            device_id={"zero": peer}, device_id_type=MESH,
        )
        copy.start()
    slot = bank * 2 + half
    for to_bank, to_zero in nearby:
        pltpu.make_async_remote_copy(
            near_out, near_in.at[slot], near_sem.at[0], near_sem.at[1],
            device_id={"bank": to_bank, "zero": to_zero}, device_id_type=MESH,
        ).start()
    near_in[slot] = near_out[...]
    part_in[me] = part[me]
    wait_for(part_in.at[pl.ds(0, PEERS - 1)], part_sem.at[1])
    summed = part_in[0]
    for n in range(1, PEERS):
        summed = summed + part_in[n]
    total[me] = summed
    for peer in peers:
        pltpu.make_async_remote_copy(
            total.at[me], total.at[me], total_sem.at[0], total_sem.at[1],
            device_id={"zero": peer}, device_id_type=MESH,
        ).start()

    wait_for(near_in.at[pl.ds(0, 7)], near_sem.at[1])
    low = lax.broadcasted_iota(jnp.int32, (16, 128), 1) < 64
    for b in range(4):
        even, odd = near_in[2 * b].astype(F32), near_in[2 * b + 1].astype(F32)
        far_out[pl.ds(16 * b, 16), :] = jnp.where(low, even, odd).astype(BF16)
    for offset, peer in zip(ORDER, peers):
        if offset[0] == 0:
            pltpu.make_async_remote_copy(
                far_out, far_in.at[me // 2], far_sem.at[0], far_sem.at[1],
                device_id={"zero": peer}, device_id_type=MESH,
            ).start()
    far_in[me // 2] = far_out[...]

    wait_for(total.at[pl.ds(0, PEERS - 1)], total_sem.at[1])
    wait_for(total.at[pl.ds(0, PEERS - 1)], total_sem.at[0])
    wait_for(part.at[pl.ds(0, PEERS - 1)], part_sem.at[0])
    for out, t in ((out_scale_gate, 0), (out_scale_up, 1)):
        for g in range(2):
            tile = total[4 * (me // 4) + 2 * t + g] / D_MODEL
            shifted = pltpu.roll(tile, lax.rem(128 - SHARE * lax.rem(me, 4), 128), 1)
            out[pl.ds(8 * g, 8), :] = shifted[:, :SHARE]
    for n in range(PEERS):
        part[n] = 1.0 / (total[n] / D_MODEL)

    for t in range(2):

        def send_step(q, carry, t=t):
            c = t * 4 + q
            for j in range(8):
                for p in range(2):
                    blocks = []
                    for h in range(2):
                        e = q * 4 + p * 2 + h
                        line = t * EXPERTS + e
                        factor = part[4 * j + line // 8, pl.ds(lax.rem(line, 8), 1), :]
                        rows = pl.ds(pl.multiple_of(e * ROWS, ROWS), ROWS)
                        blocks.append(fresh[t, rows, j * 128 : j * 128 + 128] * factor)
                    block = jnp.concatenate(blocks, axis=0)
                    narrow[c, j * 128 : j * 128 + 128, p * 128 : p * 128 + 128] = block.T.astype(BF16)
            for peer in peers:
                pltpu.make_async_remote_copy(
                    narrow.at[c, pl.ds(pl.multiple_of(peer * SHARE, SHARE), SHARE)],
                    landed.at[c, me], bulk_send.at[c], bulk_recv.at[c],
                    device_id={"zero": peer}, device_id_type=MESH,
                ).start()
            landed[c, me] = narrow[c, pl.ds(pl.multiple_of(me * SHARE, SHARE), SHARE), :]
            return carry

        lax.fori_loop(0, 4, send_step, 0)

    wait_for(far_in.at[pl.ds(0, 15)], far_sem.at[1])
    for k in range(16):
        out_router[:, k * 128 : k * 128 + 128] = far_in[k]

    for t, out in ((0, out_gate), (1, out_up)):

        def place_step(q, carry, t=t, out=out):
            c = t * 4 + q
            wait_for(landed.at[c, pl.ds(0, PEERS - 1)], bulk_recv.at[c])
            for k in range(16):
                for p in range(2):
                    lanes = slice(p * 128, p * 128 + 128)
                    even, odd = landed[c, 2 * k, :, lanes], landed[c, 2 * k + 1, :, lanes]
                    e = q * 4 + p * 2
                    to = slice(k * 128, k * 128 + 128)
                    out[e, :, to] = jnp.concatenate([even[:, :64], odd[:, :64]], axis=1)
                    out[e + 1, :, to] = jnp.concatenate([even[:, 64:], odd[:, 64:]], axis=1)
            return carry

        lax.fori_loop(0, 4, place_step, 0)

    for c in range(8):
        wait_for(landed.at[c, pl.ds(0, PEERS - 1)], bulk_send.at[c])
    wait_for(near_in.at[pl.ds(0, 7)], near_sem.at[0])
    wait_for(far_in.at[pl.ds(0, 15)], far_sem.at[0])


def on_device(w_gate, avg_gate, w_up, avg_up, mix_share, router_weight, router_gain):
    flat = [a.reshape(EXPERTS * ROWS, WIDTH) for a in (w_gate, avg_gate, w_up, avg_up)]
    vmem = pl.BlockSpec(memory_space=pltpu.VMEM)
    gate, up, scale_gate, scale_up, router = pl.pallas_call(
        kernel,
        out_shape=(
            jax.ShapeDtypeStruct((EXPERTS, SHARE, D_MODEL), BF16),
            jax.ShapeDtypeStruct((EXPERTS, SHARE, D_MODEL), BF16),
            jax.ShapeDtypeStruct((EXPERTS, SHARE), F32),
            jax.ShapeDtypeStruct((EXPERTS, SHARE), F32),
            jax.ShapeDtypeStruct((4 * EXPERTS, D_MODEL), BF16),
        ),
        in_specs=[pl.BlockSpec(memory_space=pltpu.SMEM), vmem, vmem]
        + [pl.BlockSpec(memory_space=pl.ANY)] * 4,
        out_specs=(vmem,) * 5,
        scratch_shapes=[
            pltpu.VMEM((2, EXPERTS * ROWS, WIDTH), F32),
            pltpu.VMEM((2, EXPERTS * ROWS, WIDTH), F32),
            pltpu.VMEM((PEERS, 8, 128), F32),
            pltpu.VMEM((PEERS, 8, 128), F32),
            pltpu.VMEM((PEERS, 8, 128), F32),
            pltpu.VMEM((8, WIDTH, 256), BF16),
            pltpu.VMEM((8, PEERS, SHARE, 256), BF16),
            pltpu.VMEM((16, 128), BF16),
            pltpu.VMEM((8, 16, 128), BF16),
            pltpu.VMEM((64, 128), BF16),
            pltpu.VMEM((16, 64, 128), BF16),
            pltpu.SemaphoreType.DMA((16,)),
            pltpu.SemaphoreType.DMA((2,)),
            pltpu.SemaphoreType.DMA((2,)),
            pltpu.SemaphoreType.DMA((8,)),
            pltpu.SemaphoreType.DMA((8,)),
            pltpu.SemaphoreType.DMA((2,)),
            pltpu.SemaphoreType.DMA((2,)),
        ],
        compiler_params=pltpu.CompilerParams(collective_id=0, has_side_effects=True),
        name="exchange",
    )(mix_share, router_weight.T, router_gain.reshape(1, ROWS), *flat)
    return (
        jnp.swapaxes(gate, 1, 2),
        jnp.swapaxes(up, 1, 2),
        scale_gate,
        scale_up,
        router.T,
    )


def solution(mesh):
    in_specs = (
        P("bank", "zero", None),
        P("bank", "zero", None),
        P("bank", "zero", None),
        P("bank", "zero", None),
        P("bank"),
        P("zero", "bank"),
        P("zero"),
    )
    out_specs = (
        P("bank", None, "zero"),
        P("bank", None, "zero"),
        P("bank", "zero"),
        P("bank", "zero"),
        P(),
    )
    return jax.shard_map(
        on_device, mesh=mesh, in_specs=in_specs, out_specs=out_specs, check_vma=False
    )
```

time: 183 us -> 82.3 us (0.45)
  Pallas kernels: 0 us -> 74.9 us
  local copies, waits for them, and re-layouts: 70.7 us -> 6.54 us
  waiting for transfers between devices: 57.8 us -> 0 us
  starting transfers between devices: 34.1 us -> 0 us
  other arithmetic: 17.7 us -> 0 us
    pallas_call x0 -> x1, Pallas kernels: none -> 74.9 us  [on_device(): pl.pallas_call(kernel, out_shape=(jax.ShapeDtypeStruct((EXPERTS, SHARE, D...]
    all_to_all x6 -> x0, waiting for transfers between devices: 57.8 us -> none  [the longest x3 19.6 us: from_everyone(): return lax.all_to_all(copies, axis, split_axis=0, concat_axis=0, tiled=True)]
    all_to_all x6 -> x0, starting transfers between devices: 34.1 us -> none  [the longest x3 11.1 us: from_everyone(): return lax.all_to_all(copies, axis, split_axis=0, concat_axis=0, tiled=True)]
    all_to_all x6 -> x0, local copies, waits for them, and re-layouts: 28 us -> none  [the longest x2 13.6 us: on_device(): lax.all_to_all(narrow_gate, 'zero', split_axis=2, concat_axis=1, tiled=True)]
    unnamed x15 -> x13, local copies, waits for them, and re-layouts: 29.3 us -> 6.54 us
    convert_element_type x2 -> x0, local copies, waits for them, and re-layouts: 11.1 us -> none  [the longest x1 6.2 us: on_device(): (fresh_up / jnp.expand_dims(scale_up, 1)).astype(jnp.bfloat16)]
    reduce_sum x2 -> x0, other arithmetic: 8.54 us -> none  [the longest x1 8.45 us: on_device(): jnp.sum(jnp.abs(fresh_gate), axis=1)]
    convert_element_type x2 -> x0, other arithmetic: 8.31 us -> none  [the longest x1 8.31 us: on_device(): (fresh_up / jnp.expand_dims(scale_up, 1)).astype(jnp.bfloat16)]
  transfers between devices with their start and end apart: 6 -> 0, of which waited for: 5 -> 0; matrix products, arithmetic and copies ran while one was open for 27% -> 0% of each run, Pallas kernels for 0% -> 0%
where the time goes in v1:
time: 82.3 us; the launch traced here: 82.1 us
  Pallas kernels  74.9 us (91%)
  local copies, waits for them, and re-layouts  6.54 us (8%)
    pallas_call x1, Pallas kernels, on_device(): pl.pallas_call(kernel, out_shape=(jax.ShapeDtypeStruct((EXPERTS, SHARE, D...  74.9 us
    unnamed x13, local copies, waits for them, and re-layouts  6.54 us

profile of v1, /device:TPU:0, one launch (start us, length us, event | category | flops | bytes accessed | tf_op | source)
XLA Modules:
  0.0 82.1 jit_solution(14337046186567417932)
XLA Ops:
  0.6 74.9 %exchange.1 = (bf16[16,32,2048]{2,1,0:T(8,128)(2,1)}, bf16[16,32,2048]{2,1,0:T(8,128)(2,1)}, f32[16,32]{1,0:T(8,128)}, f32[16,32]{1,0:T(8,128)}, bf16[64,2048]{1,0:T(8,128)(2,1)}) custom-call(f32[16]{0:T(128)} %mix_ref.1, f32[16,64]{1,0:T(8,128)} %bitcast.16, f32[1,64]{1,0:T(1,128)} %bitcast.17, f32[1024,1024]{1,0:T(8,128)} %bitcast.9, ...), custom_call_target="tpu_custom_call" | custom-call | tf_op jit(solution)/shard_map/exchange/pallas_call | solution.py:248
  75.5 0.0 copy-start
  75.5 0.0 copy-start.3
  75.6 0.0 copy-start.2
  75.6 0.0 copy-start.1
  75.6 3.3 %copy.17 = bf16[16,2048,32]{1,2,0:T(8,128)(2,1)} copy(bf16[16,2048,32]{1,2,0:T(8,128)(2,1)} %bitcast.14) | data formatting | bytes 4194304
  78.9 0.0 copy-done
  78.9 1.3 %copy.18 = bf16[16,2048,32]{1,2,0:T(8,128)(2,1)} copy(bf16[16,2048,32]{1,2,0:T(8,128)(2,1)S(1)} %bitcast.13) | data formatting | bytes 4194304
  80.2 0.0 copy-done.3
  80.2 0.6 copy.19
  80.8 0.0 copy-done.2
  80.8 0.6 copy.20
  81.4 0.0 copy-done.1
  81.4 0.7 copy.21
Async XLA Ops:
  75.5 3.4 %copy-start = (bf16[16,32,2048]{2,1,0:T(8,128)(2,1)S(1)}, bf16[16,32,2048]{2,1,0:T(8,128)(2,1)}, u32[]{:S(2)}) copy-start(bf16[16,32,2048]{2,1,0:T(8,128)(2,1)} %get-tuple-element.11) | copy-start | bytes 6291460
  75.5 4.7 %copy-start.3 = (f32[16,32]{1,0:T(8,128)S(1)}, f32[16,32]{1,0:T(8,128)}, u32[]{:S(2)}) copy-start(f32[16,32]{1,0:T(8,128)} %get-tuple-element.22) | copy-start | bytes 6148
  75.6 5.3 %copy-start.2 = (f32[16,32]{1,0:T(8,128)S(1)}, f32[16,32]{1,0:T(8,128)}, u32[]{:S(2)}) copy-start(f32[16,32]{1,0:T(8,128)} %get-tuple-element.23) | copy-start | bytes 6148
  75.6 5.8 %copy-start.1 = (bf16[64,2048]{1,0:T(8,128)(2,1)S(1)}, bf16[64,2048]{1,0:T(8,128)(2,1)}, u32[]{:S(2)}) copy-start(bf16[64,2048]{1,0:T(8,128)(2,1)} %get-tuple-element.14) | copy-start | bytes 786436

commit v2 on v1

--- a/solution.py
+++ b/solution.py
@@ -35,6 +35,7 @@
 
 
 ORDER = peer_order()
+FAR_FIRST = sorted(ORDER, key=lambda o: -(2 * o[0] + min(o[1], 4 - o[1]) + min(o[2], 4 - o[2])))
 
 
 def place(me, offset):
@@ -191,7 +192,7 @@
 
     for t in range(2):
 
-        def send_step(q, carry, t=t):
+        def send_step(q, carry, t=t, order=peers):
             c = t * 4 + q
             for j in range(8):
                 for p in range(2):
@@ -204,7 +205,7 @@
                         blocks.append(fresh[t, rows, j * 128 : j * 128 + 128] * factor)
                     block = jnp.concatenate(blocks, axis=0)
                     narrow[c, j * 128 : j * 128 + 128, p * 128 : p * 128 + 128] = block.T.astype(BF16)
-            for peer in peers:
+            for peer in order:
                 pltpu.make_async_remote_copy(
                     narrow.at[c, pl.ds(pl.multiple_of(peer * SHARE, SHARE), SHARE)],
                     landed.at[c, me], bulk_send.at[c], bulk_recv.at[c],
@@ -213,7 +214,9 @@
             landed[c, me] = narrow[c, pl.ds(pl.multiple_of(me * SHARE, SHARE), SHARE), :]
             return carry
 
-        lax.fori_loop(0, 4, send_step, 0)
+        lax.fori_loop(0, 4 - t, send_step, 0)
+        if t == 1:
+            send_step(3, 0, order=[place(me, o) for o in FAR_FIRST])
 
     wait_for(far_in.at[pl.ds(0, 15)], far_sem.at[1])
     for k in range(16):
@@ -242,20 +245,30 @@
     wait_for(far_in.at[pl.ds(0, 15)], far_sem.at[0])
 
 
+def write_out(*refs):
+    sources, targets, sems = refs[:5], refs[5:10], refs[10]
+    copies = [pltpu.make_async_copy(*pair, sems.at[n]) for n, pair in enumerate(zip(sources, targets))]
+    for copy in copies:
+        copy.start()
+    for copy in copies:
+        copy.wait()
+
+
 def on_device(w_gate, avg_gate, w_up, avg_up, mix_share, router_weight, router_gain):
     flat = [a.reshape(EXPERTS * ROWS, WIDTH) for a in (w_gate, avg_gate, w_up, avg_up)]
     vmem = pl.BlockSpec(memory_space=pltpu.VMEM)
-    gate, up, scale_gate, scale_up, router = pl.pallas_call(
+    results = (
+        ((EXPERTS, SHARE, D_MODEL), BF16),
+        ((EXPERTS, SHARE, D_MODEL), BF16),
+        ((EXPERTS, SHARE), F32),
+        ((EXPERTS, SHARE), F32),
+        ((4 * EXPERTS, D_MODEL), BF16),
+    )
+    held = pl.pallas_call(
         kernel,
-        out_shape=(
-            jax.ShapeDtypeStruct((EXPERTS, SHARE, D_MODEL), BF16),
-            jax.ShapeDtypeStruct((EXPERTS, SHARE, D_MODEL), BF16),
-            jax.ShapeDtypeStruct((EXPERTS, SHARE), F32),
-            jax.ShapeDtypeStruct((EXPERTS, SHARE), F32),
-            jax.ShapeDtypeStruct((4 * EXPERTS, D_MODEL), BF16),
-        ),
+        out_shape=tuple(pltpu.VMEM(*r) for r in results),
         in_specs=[pl.BlockSpec(memory_space=pltpu.SMEM), vmem, vmem]
-        + [pl.BlockSpec(memory_space=pl.ANY)] * 4,
+        + [pl.BlockSpec(memory_space=pltpu.HBM)] * 4,
         out_specs=(vmem,) * 5,
         scratch_shapes=[
             pltpu.VMEM((2, EXPERTS * ROWS, WIDTH), F32),
@@ -277,9 +290,20 @@
             pltpu.SemaphoreType.DMA((2,)),
             pltpu.SemaphoreType.DMA((2,)),
         ],
-        compiler_params=pltpu.CompilerParams(collective_id=0, has_side_effects=True),
+        compiler_params=pltpu.CompilerParams(
+            collective_id=0, has_side_effects=True, vmem_limit_bytes=58 * 1024 * 1024
+        ),
         name="exchange",
     )(mix_share, router_weight.T, router_gain.reshape(1, ROWS), *flat)
+    gate, up, scale_gate, scale_up, router = pl.pallas_call(
+        write_out,
+        out_shape=tuple(pltpu.HBM(*r) for r in results),
+        in_specs=[vmem] * len(results),
+        out_specs=(pl.BlockSpec(memory_space=pltpu.HBM),) * len(results),
+        scratch_shapes=[pltpu.SemaphoreType.DMA((len(results),))],
+        compiler_params=pltpu.CompilerParams(vmem_limit_bytes=16 * 1024 * 1024),
+        name="write_out",
+    )(*(pltpu.with_memory_space_constraint(a, pltpu.VMEM) for a in held))
     return (
         jnp.swapaxes(gate, 1, 2),
         jnp.swapaxes(up, 1, 2),

time: 82.3 us -> 75.2 us (0.914)
  local copies, waits for them, and re-layouts: 6.54 us -> 0 us
    unnamed x13 -> x0, local copies, waits for them, and re-layouts: 6.54 us -> none
    pallas_call x1 -> x2, Pallas kernels: 74.9 us -> 74.4 us  [the longest x1 72.3 us: on_device(): pl.pallas_call(kernel, out_shape=tuple((pltpu.VMEM(*r) for r in results))...]
where the time goes in v2:
time: 75.2 us; the launch traced here: 75.1 us
  Pallas kernels  74.4 us (99%)
    pallas_call x1, Pallas kernels, on_device(): pl.pallas_call(kernel, out_shape=tuple((pltpu.VMEM(*r) for r in results))...  72.3 us
    pallas_call x1, Pallas kernels, on_device(): pl.pallas_call(write_out, out_shape=tuple((pltpu.HBM(*r) for r in results...  2.14 us

profile of v2, /device:TPU:0, one launch (start us, length us, event | category | flops | bytes accessed | tf_op | source)
XLA Modules:
  0.0 75.1 jit_solution(3747207183103738094)
XLA Ops:
  0.6 72.3 %exchange.1 = (bf16[16,32,2048]{2,1,0:T(8,128)(2,1)S(1)}, bf16[16,32,2048]{2,1,0:T(8,128)(2,1)S(1)}, f32[16,32]{1,0:T(8,128)S(1)}, f32[16,32]{1,0:T(8,128)S(1)}, bf16[64,2048]{1,0:T(8,128)(2,1)S(1)}) custom-call(f32[16]{0:T(128)} %mix_ref.1, f32[16,64]{1,0:T(8,128)} %bitcast.13, f32[1,64]{1,0:T(1,128)} %bitcast.14, f32[1024,1024]{1,0:T(8,128)} %bitcast.9, ...), custom_call_target="tpu_custom_call" | custom-call | tf_op jit(solution)/shard_map/exchange/pallas_call | solution.py:267
  72.9 2.1 %write_out.1 = (bf16[16,32,2048]{2,1,0:T(8,128)(2,1)}, bf16[16,32,2048]{2,1,0:T(8,128)(2,1)}, f32[16,32]{1,0:T(8,128)}, f32[16,32]{1,0:T(8,128)}, bf16[64,2048]{1,0:T(8,128)(2,1)}) custom-call(bf16[16,32,2048]{2,1,0:T(8,128)(2,1)S(1)} %get-tuple-element.15.refs_0_, bf16[16,32,2048]{2,1,0:T(8,128)(2,1)S(1)} %get-tuple-element.16.refs_1_, ...), custom_call_target="tpu_custom_call" | custom-call | tf_op jit(solution)/shard_map/write_out/pallas_call | solution.py:298

commit v3 on v2

v3 whole, which is shorter than its diff:
```python
import functools

import jax
import jax.numpy as jnp
from jax import lax
from jax.experimental import pallas as pl
from jax.experimental.pallas import tpu as pltpu
from jax.sharding import PartitionSpec as P

D_MODEL = 2048
EXPERTS = 16
ROWS = 64
WIDTH = 1024
PEERS = 32
SHARE = 32
EARLY = 1
BEFORE = 3
F32 = jnp.float32
BF16 = jnp.bfloat16
MESH = pl.DeviceIdType.MESH


def peer_order():
    every = [(x, y, z) for z in range(4) for y in range(4) for x in range(2)][1:]
    along_x = [o for o in every if o[0]]
    along_y = [o for o in every if not o[0] and o[1]]
    along_z = [o for o in every if not o[0] and not o[1]]
    order = []
    while along_x or along_y or along_z:
        if along_x:
            order.append(along_x.pop(0))
        if along_y:
            order.append(along_y.pop(0))
        if along_z and (len(order) % 3 == 0 or not (along_x or along_y)):
            order.append(along_z.pop(0))
    return order


ORDER = peer_order()
FAR_FIRST = sorted(ORDER, key=lambda o: -(2 * o[0] + min(o[1], 4 - o[1]) + min(o[2], 4 - o[2])))


def place(me, offset):
    x, y, z = offset
    at_z = lax.rem(me // 8 + z, 4)
    at_y = lax.rem(lax.rem(me // 2, 4) + y, 4)
    at_x = lax.rem(lax.rem(me, 2) + x, 2)
    return at_z * 8 + at_y * 2 + at_x


def wait_for(ref, sem):
    pltpu.make_async_copy(ref, ref, sem).wait()


def kernel(
    mix_ref,
    router_ref,
    gain_ref,
    w_gate,
    avg_gate,
    w_up,
    avg_up,
    out_gate,
    out_up,
    out_scale_gate,
    out_scale_up,
    out_router,
    fresh,
    other,
    part,
    part_in,
    total,
    inverse,
    square,
    columns,
    early_out,
    early_in,
    narrow,
    landed,
    near_out,
    near_in,
    far_out,
    far_in,
    load_sem,
    part_send,
    part_recv,
    total_send,
    total_recv,
    early_send,
    early_recv,
    bulk_send,
    bulk_recv,
    near_sem,
    far_sem,
):
    me = lax.axis_index("zero")
    bank = lax.axis_index("bank")
    half = lax.rem(me, 2)
    barrier = pltpu.get_barrier_semaphore()
    peers = [place(me, o) for o in ORDER]
    far_first = [place(me, o) for o in FAR_FIRST]
    nearby = [
        (lax.rem(bank + b, 4), me + h * (1 - 2 * half))
        for b in range(4)
        for h in range(2)
        if (b, h) != (0, 0)
    ]
    for peer in far_first:
        pl.semaphore_signal(barrier, inc=1, device_id={"zero": peer}, device_id_type=MESH)
    for to_bank, to_zero in nearby:
        pl.semaphore_signal(
            barrier, inc=1, device_id={"bank": to_bank, "zero": to_zero}, device_id_type=MESH
        )

    loads = []
    for t, (w, a) in enumerate(((w_gate, avg_gate), (w_up, avg_up))):
        for q in range(4):
            rows = pl.ds(q * 256, 256)
            for n, (source, target) in enumerate(((w, fresh), (a, other))):
                copy = pltpu.make_async_copy(
                    source.at[rows], target.at[t, rows], load_sem.at[t * 8 + q * 2 + n]
                )
                copy.start()
                loads.append(copy)

    share = router_ref[...] * gain_ref[...]
    near_out[...] = jnp.concatenate([share, share], axis=1).astype(BF16)

    def mean(t, first=0, last=4):
        for q in range(first, last):
            for copy in loads[t * 8 + q * 2 : t * 8 + q * 2 + 2]:
                copy.wait()

            def mean_step(n, carry, q=q):
                e = q * 4 + n
                mix = mix_ref[e]
                rest = 1.0 - mix
                rows = pl.ds(pl.multiple_of(e * ROWS, ROWS), ROWS)
                for c in range(8):
                    lanes = slice(c * 128, c * 128 + 128)
                    value = mix * fresh[t, rows, lanes] + rest * other[t, rows, lanes]
                    fresh[t, rows, lanes] = value
                    part[t, 4 * c + q, pl.ds(n, 1), :] = jnp.sum(
                        jnp.abs(value), axis=0, keepdims=True
                    )
                return carry

            lax.fori_loop(0, 4, mean_step, 0)

    def share_parts(t):
        for peer in far_first:
            pltpu.make_async_remote_copy(
                part.at[t, peer], part_in.at[t, me], part_send.at[t], part_recv.at[t],
                device_id={"zero": peer}, device_id_type=MESH,
            ).start()
        part_in[t, me] = part[t, me]

    def share_totals(t):
        wait_for(part_in.at[t, pl.ds(0, PEERS - 1)], part_recv.at[t])
        summed = part_in[t, 0]
        for n in range(1, PEERS):
            summed = summed + part_in[t, n]
        total[t, me] = summed
        for peer in far_first:
            pltpu.make_async_remote_copy(
                total.at[t, me], total.at[t, me], total_send.at[t], total_recv.at[t],
                device_id={"zero": peer}, device_id_type=MESH,
            ).start()

    def take_totals(t, out):
        wait_for(total.at[t, pl.ds(0, PEERS - 1)], total_recv.at[t])
        wait_for(total.at[t, pl.ds(0, PEERS - 1)], total_send.at[t])
        for n in range(PEERS):
            inverse[t, n] = 1.0 / (total[t, n] / D_MODEL)
        turn = lax.rem(128 - SHARE * lax.rem(me, 4), 128)
        for g in range(4):
            tile = total[t, 4 * (me // 4) + g] / D_MODEL
            out[pl.ds(4 * g, 4), :] = pltpu.roll(tile, turn, 1)[:, :SHARE]

    def turned(t, pair, j, scaled):
        blocks = []
        for h in range(2):
            e = pair * 2 + h
            rows = pl.ds(pl.multiple_of(e * ROWS, ROWS), ROWS)
            block = fresh[t, rows, j * 128 : j * 128 + 128]
            if scaled:
                block = block * inverse[t, 4 * j + e // 4, pl.ds(lax.rem(e, 4), 1), :]
            blocks.append(block)
        return jnp.concatenate(blocks, axis=0).T

    def early_unit(u):
        for j in range(8):
            early_out[u, j * 128 : j * 128 + 128, :] = turned(0, u, j, False)
        early_in[u, me] = early_out[u, pl.ds(pl.multiple_of(me * SHARE, SHARE), SHARE), :]

    def early_piece(u, h):
        for peer in peers:
            pltpu.make_async_remote_copy(
                early_out.at[u, pl.ds(pl.multiple_of(peer * SHARE + h * 8, 8), 8)],
                early_in.at[u, me, pl.ds(h * 8, 8)],
                early_send.at[4 * u + h], early_recv.at[4 * u + h],
                device_id={"zero": peer}, device_id_type=MESH,
            ).start()

    def bulk_unit(t, pair, order):
        u = t * 8 + pair
        for j in range(8):
            narrow[u, j * 128 : j * 128 + 128, :] = turned(t, pair, j, True).astype(BF16)
        for peer in order:
            pltpu.make_async_remote_copy(
                narrow.at[u, pl.ds(pl.multiple_of(peer * SHARE, SHARE), SHARE)],
                landed.at[u, me], bulk_send.at[u], bulk_recv.at[u],
                device_id={"zero": peer}, device_id_type=MESH,
            ).start()
        landed[u, me] = narrow[u, pl.ds(pl.multiple_of(me * SHARE, SHARE), SHARE), :]

    def bulk(t, start, stop):
        def step(pair, carry):
            bulk_unit(t, pair, peers)
            return carry

        lax.fori_loop(start, stop, step, 0)

    mean(0, 0, 1)
    if EARLY:
        early_unit(0)
    mean(0, 1, 4)
    pl.semaphore_wait(barrier, len(peers) + len(nearby))
    share_parts(0)
    slot = bank * 2 + half
    for to_bank, to_zero in nearby:
        pltpu.make_async_remote_copy(
            near_out, near_in.at[slot], near_sem.at[0], near_sem.at[1],
            device_id={"bank": to_bank, "zero": to_zero}, device_id_type=MESH,
        ).start()
    near_in[slot] = near_out[...]
    pieces = [(u, h) for u in range(EARLY) for h in range(4)]
    for piece in pieces[:BEFORE]:
        early_piece(*piece)
    mean(1)
    share_totals(0)
    share_parts(1)
    for u in range(1, EARLY):
        early_unit(u)
    for piece in pieces[BEFORE:]:
        early_piece(*piece)

    wait_for(near_in.at[pl.ds(0, 7)], near_sem.at[1])
    low = lax.broadcasted_iota(jnp.int32, (16, 128), 1) < 64
    for b in range(4):
        even, odd = near_in[2 * b].astype(F32), near_in[2 * b + 1].astype(F32)
        far_out[pl.ds(16 * b, 16), :] = jnp.where(low, even, odd).astype(BF16)
    for offset, peer in zip(ORDER, peers):
        if offset[0] == 0:
            pltpu.make_async_remote_copy(
                far_out, far_in.at[me // 2], far_sem.at[0], far_sem.at[1],
                device_id={"zero": peer}, device_id_type=MESH,
            ).start()
    far_in[me // 2] = far_out[...]

    take_totals(0, out_scale_gate)
    bulk(0, EARLY, EARLY + 2)
    share_totals(1)
    bulk(0, EARLY + 2, 8)
    take_totals(1, out_scale_up)
    bulk(1, 0, 7)
    bulk_unit(1, 7, far_first)

    wait_for(far_in.at[pl.ds(0, 15)], far_sem.at[1])
    for k in range(16):
        out_router[:, k * 128 : k * 128 + 128] = far_in[k]

    if EARLY:
        square[...] = jnp.zeros_like(square)
        square[0:4, :] = inverse[0, 4 * (me // 4)]
        columns[...] = square[...].T
        mine = columns[pl.ds(pl.multiple_of(SHARE * lax.rem(me, 4), SHARE), SHARE), :]
    for u in range(EARLY):
        for h in range(4):
            wait_for(early_in.at[u, pl.ds(0, PEERS - 1), pl.ds(0, 8)], early_recv.at[4 * u + h])
        for k in range(16):
            even, odd = early_in[u, 2 * k], early_in[u, 2 * k + 1]
            to = slice(k * 128, k * 128 + 128)
            for h, lanes in ((0, slice(0, 64)), (1, slice(64, 128))):
                e = 2 * u + h
                row = jnp.concatenate([even[:, lanes], odd[:, lanes]], axis=1)
                out_gate[e, :, to] = (row * mine[:, e : e + 1]).astype(BF16)

    for t, out in ((0, out_gate), (1, out_up)):

        def place_step(pair, carry, t=t, out=out):
            u = t * 8 + pair
            wait_for(landed.at[u, pl.ds(0, PEERS - 1)], bulk_recv.at[u])
            for k in range(16):
                even, odd = landed[u, 2 * k], landed[u, 2 * k + 1]
                to = slice(k * 128, k * 128 + 128)
                out[pair * 2, :, to] = jnp.concatenate([even[:, :64], odd[:, :64]], axis=1)
                out[pair * 2 + 1, :, to] = jnp.concatenate([even[:, 64:], odd[:, 64:]], axis=1)
            return carry

        lax.fori_loop(EARLY * (1 - t), 8, place_step, 0)

    for u, h in pieces:
        wait_for(early_in.at[u, pl.ds(0, PEERS - 1), pl.ds(0, 8)], early_send.at[4 * u + h])
    for u in range(EARLY, 16):
        wait_for(landed.at[u, pl.ds(0, PEERS - 1)], bulk_send.at[u])
    for t in range(2):
        wait_for(part_in.at[t, pl.ds(0, PEERS - 1)], part_send.at[t])
    wait_for(near_in.at[pl.ds(0, 7)], near_sem.at[0])
    wait_for(far_in.at[pl.ds(0, 15)], far_sem.at[0])


def write_out(*refs):
    sources, targets, sems = refs[:5], refs[5:10], refs[10]
    copies = [pltpu.make_async_copy(*pair, sems.at[n]) for n, pair in enumerate(zip(sources, targets))]
    for copy in copies:
        copy.start()
    for copy in copies:
        copy.wait()


def on_device(w_gate, avg_gate, w_up, avg_up, mix_share, router_weight, router_gain):
    flat = [a.reshape(EXPERTS * ROWS, WIDTH) for a in (w_gate, avg_gate, w_up, avg_up)]
    vmem = pl.BlockSpec(memory_space=pltpu.VMEM)
    results = (
        ((EXPERTS, SHARE, D_MODEL), BF16),
        ((EXPERTS, SHARE, D_MODEL), BF16),
        ((EXPERTS, SHARE), F32),
        ((EXPERTS, SHARE), F32),
        ((4 * EXPERTS, D_MODEL), BF16),
    )
    held = pl.pallas_call(
        kernel,
        out_shape=tuple(pltpu.VMEM(*r) for r in results),
        in_specs=[pl.BlockSpec(memory_space=pltpu.SMEM), vmem, vmem]
        + [pl.BlockSpec(memory_space=pltpu.HBM)] * 4,
        out_specs=(vmem,) * 5,
        scratch_shapes=[
            pltpu.VMEM((2, EXPERTS * ROWS, WIDTH), F32),
            pltpu.VMEM((2, EXPERTS * ROWS, WIDTH), F32),
            pltpu.VMEM((2, PEERS, 4, 128), F32),
            pltpu.VMEM((2, PEERS, 4, 128), F32),
            pltpu.VMEM((2, PEERS, 4, 128), F32),
            pltpu.VMEM((2, PEERS, 4, 128), F32),
            pltpu.VMEM((128, 128), F32),
            pltpu.VMEM((128, 128), F32),
            pltpu.VMEM((max(EARLY, 1), WIDTH, 128), F32),
            pltpu.VMEM((max(EARLY, 1), PEERS, SHARE, 128), F32),
            pltpu.VMEM((16, WIDTH, 128), BF16),
            pltpu.VMEM((16, PEERS, SHARE, 128), BF16),
            pltpu.VMEM((16, 128), BF16),
            pltpu.VMEM((8, 16, 128), BF16),
            pltpu.VMEM((64, 128), BF16),
            pltpu.VMEM((16, 64, 128), BF16),
            pltpu.SemaphoreType.DMA((16,)),
            pltpu.SemaphoreType.DMA((2,)),
            pltpu.SemaphoreType.DMA((2,)),
            pltpu.SemaphoreType.DMA((2,)),
            pltpu.SemaphoreType.DMA((2,)),
            pltpu.SemaphoreType.DMA((max(4 * EARLY, 1),)),
            pltpu.SemaphoreType.DMA((max(4 * EARLY, 1),)),
            pltpu.SemaphoreType.DMA((16,)),
            pltpu.SemaphoreType.DMA((16,)),
            pltpu.SemaphoreType.DMA((2,)),
            pltpu.SemaphoreType.DMA((2,)),
        ],
        compiler_params=pltpu.CompilerParams(
            collective_id=0, has_side_effects=True, vmem_limit_bytes=58 * 1024 * 1024
        ),
        name="exchange",
    )(mix_share, router_weight.T, router_gain.reshape(1, ROWS), *flat)
    gate, up, scale_gate, scale_up, router = pl.pallas_call(
        write_out,
        out_shape=tuple(pltpu.HBM(*r) for r in results),
        in_specs=[vmem] * len(results),
        out_specs=(pl.BlockSpec(memory_space=pltpu.HBM),) * len(results),
        scratch_shapes=[pltpu.SemaphoreType.DMA((len(results),))],
        compiler_params=pltpu.CompilerParams(vmem_limit_bytes=16 * 1024 * 1024),
        name="write_out",
    )(*(pltpu.with_memory_space_constraint(a, pltpu.VMEM) for a in held))
    return (
        jnp.swapaxes(gate, 1, 2),
        jnp.swapaxes(up, 1, 2),
        scale_gate,
        scale_up,
        router.T,
    )


def solution(mesh):
    in_specs = (
        P("bank", "zero", None),
        P("bank", "zero", None),
        P("bank", "zero", None),
        P("bank", "zero", None),
        P("bank"),
        P("zero", "bank"),
        P("zero"),
    )
    out_specs = (
        P("bank", None, "zero"),
        P("bank", None, "zero"),
        P("bank", "zero"),
        P("bank", "zero"),
        P(),
    )
    return jax.shard_map(
        on_device, mesh=mesh, in_specs=in_specs, out_specs=out_specs, check_vma=False
    )
```

time: 75.2 us -> 70.8 us (0.941)
  Pallas kernels: 74.4 us -> 70 us
    pallas_call x1, Pallas kernels: 72.3 us -> 67.9 us  [on_device(): pl.pallas_call(kernel, out_shape=tuple((pltpu.VMEM(*r) for r in results))...]
where the time goes in v3:
time: 70.8 us; the launch traced here: 70.6 us
  Pallas kernels  70 us (99%)
    pallas_call x1, Pallas kernels, on_device(): pl.pallas_call(kernel, out_shape=tuple((pltpu.VMEM(*r) for r in results))...  67.9 us
    pallas_call x1, Pallas kernels, on_device(): pl.pallas_call(write_out, out_shape=tuple((pltpu.HBM(*r) for r in results...  2.14 us

profile of v3, /device:TPU:0, one launch (start us, length us, event | category | flops | bytes accessed | tf_op | source)
XLA Modules:
  0.0 70.6 jit_solution(8521605225962267574)
XLA Ops:
  0.6 67.9 %exchange.1 = (bf16[16,32,2048]{2,1,0:T(8,128)(2,1)S(1)}, bf16[16,32,2048]{2,1,0:T(8,128)(2,1)S(1)}, f32[16,32]{1,0:T(8,128)S(1)}, f32[16,32]{1,0:T(8,128)S(1)}, bf16[64,2048]{1,0:T(8,128)(2,1)S(1)}) custom-call(f32[16]{0:T(128)} %mix_ref.1, f32[16,64]{1,0:T(8,128)} %bitcast.13, f32[1,64]{1,0:T(1,128)} %bitcast.14, f32[1024,1024]{1,0:T(8,128)} %bitcast.9, ...), custom_call_target="tpu_custom_call" | custom-call | tf_op jit(solution)/shard_map/exchange/pallas_call | solution.py:332
  68.5 2.1 %write_out.1 = (bf16[16,32,2048]{2,1,0:T(8,128)(2,1)}, bf16[16,32,2048]{2,1,0:T(8,128)(2,1)}, f32[16,32]{1,0:T(8,128)}, f32[16,32]{1,0:T(8,128)}, bf16[64,2048]{1,0:T(8,128)(2,1)}) custom-call(bf16[16,32,2048]{2,1,0:T(8,128)(2,1)S(1)} %get-tuple-element.15.refs_0_, bf16[16,32,2048]{2,1,0:T(8,128)(2,1)S(1)} %get-tuple-element.16.refs_1_, ...), custom_call_target="tpu_custom_call" | custom-call | tf_op jit(solution)/shard_map/write_out/pallas_call | solution.py:372

commit v4 on v3

--- a/solution.py
+++ b/solution.py
@@ -14,7 +14,6 @@
 PEERS = 32
 SHARE = 32
 EARLY = 1
-BEFORE = 3
 F32 = jnp.float32
 BF16 = jnp.bfloat16
 MESH = pl.DeviceIdType.MESH
@@ -96,6 +95,7 @@
     me = lax.axis_index("zero")
     bank = lax.axis_index("bank")
     half = lax.rem(me, 2)
+    tile = me // 2
     barrier = pltpu.get_barrier_semaphore()
     peers = [place(me, o) for o in ORDER]
     far_first = [place(me, o) for o in FAR_FIRST]
@@ -105,7 +105,9 @@
         for h in range(2)
         if (b, h) != (0, 0)
     ]
-    for peer in far_first:
+    plane = [place(me, o) for o in FAR_FIRST if o[0] == 0]
+    across = [place(me, o) for o in FAR_FIRST if o[0] == 1]
+    for peer in plane:
         pl.semaphore_signal(barrier, inc=1, device_id={"zero": peer}, device_id_type=MESH)
     for to_bank, to_zero in nearby:
         pl.semaphore_signal(
@@ -140,7 +142,7 @@
                     lanes = slice(c * 128, c * 128 + 128)
                     value = mix * fresh[t, rows, lanes] + rest * other[t, rows, lanes]
                     fresh[t, rows, lanes] = value
-                    part[t, 4 * c + q, pl.ds(n, 1), :] = jnp.sum(
+                    part[t, 2 * c + e // 8, pl.ds(lax.rem(e, 8), 1), :] = jnp.sum(
                         jnp.abs(value), axis=0, keepdims=True
                     )
                 return carry
@@ -148,17 +150,17 @@
             lax.fori_loop(0, 4, mean_step, 0)
 
     def share_parts(t):
-        for peer in far_first:
+        for peer in plane:
             pltpu.make_async_remote_copy(
-                part.at[t, peer], part_in.at[t, me], part_send.at[t], part_recv.at[t],
+                part.at[t, peer // 2], part_in.at[t, tile], part_send.at[t], part_recv.at[t],
                 device_id={"zero": peer}, device_id_type=MESH,
             ).start()
-        part_in[t, me] = part[t, me]
+        part_in[t, tile] = part[t, tile]
 
     def share_totals(t):
-        wait_for(part_in.at[t, pl.ds(0, PEERS - 1)], part_recv.at[t])
+        wait_for(part_in.at[t, pl.ds(0, 15)], part_recv.at[t])
         summed = part_in[t, 0]
-        for n in range(1, PEERS):
+        for n in range(1, 16):
             summed = summed + part_in[t, n]
         total[t, me] = summed
         for peer in far_first:
@@ -170,12 +172,13 @@
     def take_totals(t, out):
         wait_for(total.at[t, pl.ds(0, PEERS - 1)], total_recv.at[t])
         wait_for(total.at[t, pl.ds(0, PEERS - 1)], total_send.at[t])
-        for n in range(PEERS):
-            inverse[t, n] = 1.0 / (total[t, n] / D_MODEL)
+        for n in range(16):
+            total[t, 2 * n] = (total[t, 2 * n] + total[t, 2 * n + 1]) / D_MODEL
+            inverse[t, n] = 1.0 / total[t, 2 * n]
         turn = lax.rem(128 - SHARE * lax.rem(me, 4), 128)
-        for g in range(4):
-            tile = total[t, 4 * (me // 4) + g] / D_MODEL
-            out[pl.ds(4 * g, 4), :] = pltpu.roll(tile, turn, 1)[:, :SHARE]
+        for g in range(2):
+            scale = total[t, 2 * (2 * (me // 4) + g)]
+            out[pl.ds(8 * g, 8), :] = pltpu.roll(scale, turn, 1)[:, :SHARE]
 
     def turned(t, pair, j, scaled):
         blocks = []
@@ -184,7 +187,7 @@
             rows = pl.ds(pl.multiple_of(e * ROWS, ROWS), ROWS)
             block = fresh[t, rows, j * 128 : j * 128 + 128]
             if scaled:
-                block = block * inverse[t, 4 * j + e // 4, pl.ds(lax.rem(e, 4), 1), :]
+                block = block * inverse[t, 2 * j + e // 8, pl.ds(lax.rem(e, 8), 1), :]
             blocks.append(block)
         return jnp.concatenate(blocks, axis=0).T
 
@@ -193,12 +196,11 @@
             early_out[u, j * 128 : j * 128 + 128, :] = turned(0, u, j, False)
         early_in[u, me] = early_out[u, pl.ds(pl.multiple_of(me * SHARE, SHARE), SHARE), :]
 
-    def early_piece(u, h):
-        for peer in peers:
+    def early_send_to(u, group):
+        for peer in group:
             pltpu.make_async_remote_copy(
-                early_out.at[u, pl.ds(pl.multiple_of(peer * SHARE + h * 8, 8), 8)],
-                early_in.at[u, me, pl.ds(h * 8, 8)],
-                early_send.at[4 * u + h], early_recv.at[4 * u + h],
+                early_out.at[u, pl.ds(pl.multiple_of(peer * SHARE, SHARE), SHARE)],
+                early_in.at[u, me], early_send.at[u], early_recv.at[u],
                 device_id={"zero": peer}, device_id_type=MESH,
             ).start()
 
@@ -225,7 +227,7 @@
     if EARLY:
         early_unit(0)
     mean(0, 1, 4)
-    pl.semaphore_wait(barrier, len(peers) + len(nearby))
+    pl.semaphore_wait(barrier, len(plane) + len(nearby))
     share_parts(0)
     slot = bank * 2 + half
     for to_bank, to_zero in nearby:
@@ -234,16 +236,16 @@
             device_id={"bank": to_bank, "zero": to_zero}, device_id_type=MESH,
         ).start()
     near_in[slot] = near_out[...]
-    pieces = [(u, h) for u in range(EARLY) for h in range(4)]
-    for piece in pieces[:BEFORE]:
-        early_piece(*piece)
+    if EARLY:
+        early_send_to(0, plane)
     mean(1)
     share_totals(0)
     share_parts(1)
-    for u in range(1, EARLY):
-        early_unit(u)
-    for piece in pieces[BEFORE:]:
-        early_piece(*piece)
+    for u in range(EARLY):
+        if u:
+            early_unit(u)
+            early_send_to(u, plane)
+        early_send_to(u, across)
 
     wait_for(near_in.at[pl.ds(0, 7)], near_sem.at[1])
     low = lax.broadcasted_iota(jnp.int32, (16, 128), 1) < 64
@@ -272,12 +274,11 @@
 
     if EARLY:
         square[...] = jnp.zeros_like(square)
-        square[0:4, :] = inverse[0, 4 * (me // 4)]
+        square[0:8, :] = inverse[0, 2 * (me // 4)]
         columns[...] = square[...].T
         mine = columns[pl.ds(pl.multiple_of(SHARE * lax.rem(me, 4), SHARE), SHARE), :]
     for u in range(EARLY):
-        for h in range(4):
-            wait_for(early_in.at[u, pl.ds(0, PEERS - 1), pl.ds(0, 8)], early_recv.at[4 * u + h])
+        wait_for(early_in.at[u, pl.ds(0, PEERS - 1)], early_recv.at[u])
         for k in range(16):
             even, odd = early_in[u, 2 * k], early_in[u, 2 * k + 1]
             to = slice(k * 128, k * 128 + 128)
@@ -300,12 +301,12 @@
 
         lax.fori_loop(EARLY * (1 - t), 8, place_step, 0)
 
-    for u, h in pieces:
-        wait_for(early_in.at[u, pl.ds(0, PEERS - 1), pl.ds(0, 8)], early_send.at[4 * u + h])
+    for u in range(EARLY):
+        wait_for(early_in.at[u, pl.ds(0, PEERS - 1)], early_send.at[u])
     for u in range(EARLY, 16):
         wait_for(landed.at[u, pl.ds(0, PEERS - 1)], bulk_send.at[u])
     for t in range(2):
-        wait_for(part_in.at[t, pl.ds(0, PEERS - 1)], part_send.at[t])
+        wait_for(part_in.at[t, pl.ds(0, 15)], part_send.at[t])
     wait_for(near_in.at[pl.ds(0, 7)], near_sem.at[0])
     wait_for(far_in.at[pl.ds(0, 15)], far_sem.at[0])
 
@@ -338,10 +339,10 @@
         scratch_shapes=[
             pltpu.VMEM((2, EXPERTS * ROWS, WIDTH), F32),
             pltpu.VMEM((2, EXPERTS * ROWS, WIDTH), F32),
-            pltpu.VMEM((2, PEERS, 4, 128), F32),
-            pltpu.VMEM((2, PEERS, 4, 128), F32),
-            pltpu.VMEM((2, PEERS, 4, 128), F32),
-            pltpu.VMEM((2, PEERS, 4, 128), F32),
+            pltpu.VMEM((2, 16, 8, 128), F32),
+            pltpu.VMEM((2, 16, 8, 128), F32),
+            pltpu.VMEM((2, PEERS, 8, 128), F32),
+            pltpu.VMEM((2, 16, 8, 128), F32),
             pltpu.VMEM((128, 128), F32),
             pltpu.VMEM((128, 128), F32),
             pltpu.VMEM((max(EARLY, 1), WIDTH, 128), F32),
@@ -357,8 +358,8 @@
             pltpu.SemaphoreType.DMA((2,)),
             pltpu.SemaphoreType.DMA((2,)),
             pltpu.SemaphoreType.DMA((2,)),
-            pltpu.SemaphoreType.DMA((max(4 * EARLY, 1),)),
-            pltpu.SemaphoreType.DMA((max(4 * EARLY, 1),)),
+            pltpu.SemaphoreType.DMA((max(EARLY, 1),)),
+            pltpu.SemaphoreType.DMA((max(EARLY, 1),)),
             pltpu.SemaphoreType.DMA((16,)),
             pltpu.SemaphoreType.DMA((16,)),
             pltpu.SemaphoreType.DMA((2,)),

time: 70.8 us -> 71 us (level)
  no operation moved by 1% of the time
where the time goes in v4:
time: 71 us; the launch traced here: 70.9 us
  Pallas kernels  70.2 us (99%)
    pallas_call x1, Pallas kernels, on_device(): pl.pallas_call(kernel, out_shape=tuple((pltpu.VMEM(*r) for r in results))...  68.1 us
    pallas_call x1, Pallas kernels, on_device(): pl.pallas_call(write_out, out_shape=tuple((pltpu.HBM(*r) for r in results...  2.14 us

profile of v4, /device:TPU:0, one launch (start us, length us, event | category | flops | bytes accessed | tf_op | source)
XLA Modules:
  0.0 70.9 jit_solution(8609915876088557884)
XLA Ops:
  0.6 68.1 %exchange.1 = (bf16[16,32,2048]{2,1,0:T(8,128)(2,1)S(1)}, bf16[16,32,2048]{2,1,0:T(8,128)(2,1)S(1)}, f32[16,32]{1,0:T(8,128)S(1)}, f32[16,32]{1,0:T(8,128)S(1)}, bf16[64,2048]{1,0:T(8,128)(2,1)S(1)}) custom-call(f32[16]{0:T(128)} %mix_ref.1, f32[16,64]{1,0:T(8,128)} %bitcast.13, f32[1,64]{1,0:T(1,128)} %bitcast.14, f32[1024,1024]{1,0:T(8,128)} %bitcast.9, ...), custom_call_target="tpu_custom_call" | custom-call | tf_op jit(solution)/shard_map/exchange/pallas_call | solution.py:333
  68.7 2.1 %write_out.1 = (bf16[16,32,2048]{2,1,0:T(8,128)(2,1)}, bf16[16,32,2048]{2,1,0:T(8,128)(2,1)}, f32[16,32]{1,0:T(8,128)}, f32[16,32]{1,0:T(8,128)}, bf16[64,2048]{1,0:T(8,128)(2,1)}) custom-call(bf16[16,32,2048]{2,1,0:T(8,128)(2,1)S(1)} %get-tuple-element.15.refs_0_, bf16[16,32,2048]{2,1,0:T(8,128)(2,1)S(1)} %get-tuple-element.16.refs_1_, ...), custom_call_target="tpu_custom_call" | custom-call | tf_op jit(solution)/shard_map/write_out/pallas_call | solution.py:373

commit v5 on v3

--- a/solution.py
+++ b/solution.py
@@ -14,7 +14,7 @@
 PEERS = 32
 SHARE = 32
 EARLY = 1
-BEFORE = 3
+BEFORE = 2
 F32 = jnp.float32
 BF16 = jnp.bfloat16
 MESH = pl.DeviceIdType.MESH
@@ -92,6 +92,7 @@
     bulk_recv,
     near_sem,
     far_sem,
+    swap_sem,
 ):
     me = lax.axis_index("zero")
     bank = lax.axis_index("bank")
@@ -167,11 +168,13 @@
                 device_id={"zero": peer}, device_id_type=MESH,
             ).start()
 
-    def take_totals(t, out):
+    def take_totals(t):
         wait_for(total.at[t, pl.ds(0, PEERS - 1)], total_recv.at[t])
-        wait_for(total.at[t, pl.ds(0, PEERS - 1)], total_send.at[t])
         for n in range(PEERS):
             inverse[t, n] = 1.0 / (total[t, n] / D_MODEL)
+
+    def give_scales(t, out):
+        wait_for(total.at[t, pl.ds(0, PEERS - 1)], total_send.at[t])
         turn = lax.rem(128 - SHARE * lax.rem(me, 4), 128)
         for g in range(4):
             tile = total[t, 4 * (me // 4) + g] / D_MODEL
@@ -250,23 +253,32 @@
     for b in range(4):
         even, odd = near_in[2 * b].astype(F32), near_in[2 * b + 1].astype(F32)
         far_out[pl.ds(16 * b, 16), :] = jnp.where(low, even, odd).astype(BF16)
+    core = lax.rem(bank, 2)
+    own_rows = pl.ds(pl.multiple_of(32 * core, 32), 32)
     for offset, peer in zip(ORDER, peers):
         if offset[0] == 0:
             pltpu.make_async_remote_copy(
-                far_out, far_in.at[me // 2], far_sem.at[0], far_sem.at[1],
+                far_out.at[own_rows], far_in.at[me // 2, own_rows], far_sem.at[0], far_sem.at[1],
                 device_id={"zero": peer}, device_id_type=MESH,
             ).start()
-    far_in[me // 2] = far_out[...]
-
-    take_totals(0, out_scale_gate)
+    far_in[me // 2, own_rows, :] = far_out[own_rows, :]
+
+    take_totals(0)
     bulk(0, EARLY, EARLY + 2)
     share_totals(1)
     bulk(0, EARLY + 2, 8)
-    take_totals(1, out_scale_up)
+    take_totals(1)
     bulk(1, 0, 7)
     bulk_unit(1, 7, far_first)
-
-    wait_for(far_in.at[pl.ds(0, 15)], far_sem.at[1])
+    give_scales(0, out_scale_gate)
+    give_scales(1, out_scale_up)
+
+    wait_for(far_in.at[pl.ds(0, 15), pl.ds(0, 32)], far_sem.at[1])
+    pltpu.make_async_remote_copy(
+        far_in.at[:, own_rows], far_in.at[:, own_rows], swap_sem.at[0], swap_sem.at[1],
+        device_id={"bank": bank + 1 - 2 * core, "zero": me}, device_id_type=MESH,
+    ).start()
+    wait_for(far_in.at[:, pl.ds(0, 32)], swap_sem.at[1])
     for k in range(16):
         out_router[:, k * 128 : k * 128 + 128] = far_in[k]
 
@@ -307,7 +319,8 @@
     for t in range(2):
         wait_for(part_in.at[t, pl.ds(0, PEERS - 1)], part_send.at[t])
     wait_for(near_in.at[pl.ds(0, 7)], near_sem.at[0])
-    wait_for(far_in.at[pl.ds(0, 15)], far_sem.at[0])
+    wait_for(far_in.at[pl.ds(0, 15), pl.ds(0, 32)], far_sem.at[0])
+    wait_for(far_in.at[:, pl.ds(0, 32)], swap_sem.at[0])
 
 
 def write_out(*refs):
@@ -363,6 +376,7 @@
             pltpu.SemaphoreType.DMA((16,)),
             pltpu.SemaphoreType.DMA((2,)),
             pltpu.SemaphoreType.DMA((2,)),
+            pltpu.SemaphoreType.DMA((2,)),
         ],
         compiler_params=pltpu.CompilerParams(
             collective_id=0, has_side_effects=True, vmem_limit_bytes=58 * 1024 * 1024

time: 70.8 us -> 70.7 us (level)
  no operation moved by 1% of the time
where the time goes in v5:
time: 70.7 us; the launch traced here: 70.5 us
  Pallas kernels  69.9 us (99%)
    pallas_call x1, Pallas kernels, on_device(): pl.pallas_call(kernel, out_shape=tuple((pltpu.VMEM(*r) for r in results))...  67.8 us
    pallas_call x1, Pallas kernels, on_device(): pl.pallas_call(write_out, out_shape=tuple((pltpu.HBM(*r) for r in results...  2.14 us

profile of v5, /device:TPU:0, one launch (start us, length us, event | category | flops | bytes accessed | tf_op | source)
XLA Modules:
  0.0 70.5 jit_solution(4913059356676130680)
XLA Ops:
  0.6 67.8 %exchange.1 = (bf16[16,32,2048]{2,1,0:T(8,128)(2,1)S(1)}, bf16[16,32,2048]{2,1,0:T(8,128)(2,1)S(1)}, f32[16,32]{1,0:T(8,128)S(1)}, f32[16,32]{1,0:T(8,128)S(1)}, bf16[64,2048]{1,0:T(8,128)(2,1)S(1)}) custom-call(f32[16]{0:T(128)} %mix_ref.1, f32[16,64]{1,0:T(8,128)} %bitcast.13, f32[1,64]{1,0:T(1,128)} %bitcast.14, f32[1024,1024]{1,0:T(8,128)} %bitcast.9, ...), custom_call_target="tpu_custom_call" | custom-call | tf_op jit(solution)/shard_map/exchange/pallas_call | solution.py:345
  68.4 2.1 %write_out.1 = (bf16[16,32,2048]{2,1,0:T(8,128)(2,1)}, bf16[16,32,2048]{2,1,0:T(8,128)(2,1)}, f32[16,32]{1,0:T(8,128)}, f32[16,32]{1,0:T(8,128)}, bf16[64,2048]{1,0:T(8,128)(2,1)}) custom-call(bf16[16,32,2048]{2,1,0:T(8,128)(2,1)S(1)} %get-tuple-element.15.refs_0_, bf16[16,32,2048]{2,1,0:T(8,128)(2,1)S(1)} %get-tuple-element.16.refs_1_, ...), custom_call_target="tpu_custom_call" | custom-call | tf_op jit(solution)/shard_map/write_out/pallas_call | solution.py:386
